TPU v7x, 32 devices: a whole 2x2x4 slice. The times are simulated.
32 devices in a mesh: row: 8 (over z, x), col: 4 (over y, core).
Axes of the slice: x: 2, y: 2, z: 4, core: 2. Of those that a mesh axis runs over, the one named last changes fastest.
Arguments:
- prior_scores: float32 [12288, 12288], P('row', 'col'), may hold values from 0.001 to 10
- tiles_first: bfloat16 [96, 5, 128, 128], P('row'), may hold values from 0 to 1, as said below
- columns_first: int32 [96, 5], P('row'), may hold values from 0 to 95, as said below
- tiles_second: bfloat16 [96, 5, 128, 128], P('col'), may hold values from 0 to 1, as said below
- columns_second: int32 [96, 5], P('col'), may hold values from 0 to 95, as said below
Outputs:
- alignment: float32 [12288, 12288], P('row', 'col')
Inputs may be any that keep to these rules, and one draw needn't show every extreme that they name: `tiles_first`: in every block row, the block in the first slot has entries of 0.5 or more on its diagonal. `tiles_second`: in every block row, the block in the first slot has entries of 0.5 or more on its diagonal. `columns_first`: each block row lists 5 different block columns. `columns_second`: each block row lists 5 different block columns.
All inputs are finite; a program needn't handle non-finite values.
Results may differ from a plain program's by a relative error of at most 0.0004.
The roundings to bfloat16 on the way count: a program that leaves them out, or rounds other values in their place, can miss the bound.
Values may be sent and summed in bfloat16 or wider, within the bound.
A program may use at most 192 MiB of HBM per device.

v0:
```python
import jax
import jax.numpy as jnp
from jax import lax
from jax.sharding import PartitionSpec as P

ITERS = 2
mixing = 0.8


def second_product(features, tile_set, columns, inverse):
    tile_size = tile_set.shape[2]
    blocks = features.reshape(-1, tile_size, features.shape[1])
    picked = jnp.take(blocks, columns, axis=0)
    result = jnp.einsum("jsoi,jsin->jon", tile_set, picked, preferred_element_type=jnp.float32)
    result = result.reshape(-1, features.shape[1]) * inverse[:, None]
    return result.astype(jnp.bfloat16)


def first_product(slab_data, tile_set, columns, inverse):
    tile_size = tile_set.shape[2]
    blocks = slab_data.reshape(slab_data.shape[0], -1, tile_size)
    picked = jnp.take(blocks, columns, axis=1)
    result = jnp.einsum("cisk,isok->cio", picked, tile_set, preferred_element_type=jnp.float32)
    result = result.reshape(slab_data.shape[0], -1) * inverse[None, :]
    return result.astype(jnp.bfloat16)


def local(prior_scores, tiles_first, columns_first, tiles_second, columns_second):
    prior_cols = prior_scores.T
    row_count = lax.axis_size("row")
    cell_count = float(
        prior_scores.shape[0] * row_count * prior_scores.shape[1] * lax.axis_size("col")
    )
    all_first, all_columns = (
        lax.all_gather(tiles_first, "row", axis=0, tiled=True),
        lax.all_gather(columns_first, "row", axis=0, tiled=True),
    )
    inverse_first = 1.0 / jnp.sum(all_first, axis=(1, 3), dtype=jnp.float32).reshape(-1)
    inverse_second = 1.0 / jnp.sum(tiles_second, axis=(1, 3), dtype=jnp.float32).reshape(-1)
    prior_sum = lax.psum(jnp.sum(prior_cols), ("row", "col"))
    current_state = prior_cols
    for iteration in range(ITERS):
        current = current_state.astype(jnp.bfloat16)
        gathered = lax.all_gather(current, "col", axis=0, tiled=True)
        mixed_cols = second_product(gathered, tiles_second, columns_second, inverse_second)
        slab_data = lax.all_to_all(mixed_cols, "row", split_axis=0, concat_axis=1, tiled=True)
        propagated = first_product(slab_data, all_first, all_columns, inverse_first)
        partial_value = jnp.sum(propagated.astype(jnp.float32))
        returned = lax.all_to_all(propagated, "row", split_axis=1, concat_axis=0, tiled=True)
        slab_sum = lax.psum(partial_value, ("row", "col"))
        grand_total = mixing * slab_sum + (1.0 - mixing) * prior_sum
        updated = mixing * returned.astype(jnp.float32) + (1.0 - mixing) * prior_cols
        current_state = updated / (grand_total / cell_count)
    return current_state.T


def solution(mesh):
    return jax.shard_map(
        local,
        mesh=mesh,
        in_specs=(
            P("row", "col"),
            P("row", None, None, None),
            P("row", None),
            P("col", None, None, None),
            P("col", None),
        ),
        out_specs=P("row", "col"),
        check_vma=False,
    )
```

profile of v0, /device:TPU:0, one launch (start us, length us, event | category | flops | bytes accessed | tf_op | source)
XLA Modules:
  0.0 1965.2 jit_solution(3482156097374935337)
XLA Ops:
  6.5 20.0 %fusion.28 = (f32[]{:T(128)}, bf16[3072,1536]{0,1:T(8,128)(2,1)}) fusion(f32[1536,3072]{1,0:T(8,128)} %param.9), kind=kLoop, calls=%fused_computation.55 | loop fusion | flops 9437183 | bytes 28311556 | tf_op jit(solution)/shard_map/reduce_sum | solution.py:40
  30.4 226.2 %all-gather.5.cloned.1.call-done = bf16[12288,1536]{0,1:T(8,128)(2,1)} async-done(((bf16[3072,1536]{0,1:T(8,128)(2,1)}), bf16[12288,1536]{0,1:T(8,128)(2,1)}) %all-gather.5.cloned.1.call-update) | async-done | bytes 37748752 | tf_op jit(solution)/shard_map/all_gather | solution.py:44
  256.6 48.9 %copy.36 = bf16[12288,1536]{1,0:T(8,128)(2,1)} copy(bf16[12288,1536]{0,1:T(8,128)(2,1)} %all-gather.5.cloned.1.call-done) | data formatting | bytes 75497472 | tf_op jit(solution)/shard_map/all_gather | solution.py:44
  305.6 33.3 %gather_fusion = bf16[120,128,1536]{2,1,0:T(8,128)(2,1)} fusion(bf16[96,128,1536]{2,1,0:T(8,128)(2,1)} %bitcast.87, s32[1024]{0:T(1024)S(1)} %pad_clamp_fusion.1), kind=kCustom, calls=%fused_computation.clone | custom fusion | bytes 94372320 | tf_op jit(solution)/shard_map/jit(_take)/gather | solution.py:13
  338.8 26.4 %fusion.8 = f32[24,1536,128,1]{1,2,3,0:T(8,128)} fusion(bf16[24,5,128,128]{3,2,1,0:T(8,128)(2,1)} %param.12, bf16[24,5,128,1536]{3,2,1,0:T(8,128)(2,1)} %bitcast.93, pred[24,5]{1,0:T(8,128)(4,1)S(1)} %copy.33), kind=kOutput, calls=%fused_computation.12 | convolution fusion | flops 6063390720 | bytes 69992568 | tf_op jit(solution)/shard_map/jsoi,jsin->jon/dot_general | solution.py:14
  365.2 18.7 copy.38
  383.9 11.5 multiply_convert_fusion.3
  400.8 292.1 %all-gather = s32[8,12,5]{1,2,0:T(8,128)S(1)} all-gather(s32[1,12,5]{1,2,0:T(8,128)S(1)} %bitcast.99), channel_id=1, replica_groups=mesh['row'=8,'col'=4] {'row'}, dimensions={0}, use_global_device_ids=true | all-gather | bytes 2160 | tf_op jit(solution)/shard_map/all_gather | solution.py:36
  693.5 6.6 convert_reduce_fusion
  700.2 12.6 copy.40
  712.8 23.6 %gather_fusion.1 = bf16[480,384,128]{2,1,0:T(8,128)(2,1)} fusion(bf16[384,96,128]{2,0,1:T(8,128)(2,1)} %copy.40, s32[1024]{0:T(1024)S(1)} %pad_clamp_fusion), kind=kCustom, calls=%fused_computation.1.clone | custom fusion | bytes 94373760 | tf_op jit(solution)/shard_map/jit(_take)/gather | solution.py:22
  736.4 31.3 %convert_reduce_fusion.2 = (f32[]{:T(128)}, f32[96,384,128,1]{1,2,3,0:T(8,128)}) fusion(f32[96,128]{1,0:T(8,128)S(1)} %broadcast_divide_fusion, bf16[96,5,128,128]{3,2,1,0:T(8,128)(2,1)} %all-gather.7.cloned.1.call-done, bf16[96,5,384,128]{3,2,1,0:T(8,128)(2,1)} %bitcast.89, pred[96,5]{1,0:T(8,128)(4,1)S(1)} %copy.32), kind=kOutput, calls=%fused_computation.37 | convolution fusion | flops 6082265088 | bytes 81838560 | tf_op jit(solution)/shard_map/cisk,isok->cio/dot_general | solution.py:23
  767.7 11.8 multiply_convert_fusion.2
  784.6 220.6 %all-reduce = (f32[]{:T(128)}, f32[]{:T(128)}) all-reduce(f32[]{:T(128)} %get-tuple-element.11, f32[]{:T(128)} %get-tuple-element.9), channel_id=1, replica_groups=mesh['row'=8,'col'=4] {'row','col'}, use_global_device_ids=true, to_apply=%region_3.6 | all-reduce | flops 2 | bytes 16 | tf_op jit(solution)/shard_map/psum | solution.py:50
  1006.5 12.4 multiply_bitcast_fusion.1
  1018.9 7.6 copy.52
  1026.5 12.7 fusion.21
  1039.2 227.3 %all-gather.9.cloned.1.call-done = bf16[12288,1536]{0,1:T(8,128)(2,1)} async-done(((bf16[3072,1536]{0,1:T(8,128)(2,1)}), bf16[12288,1536]{0,1:T(8,128)(2,1)}) %all-gather.9.cloned.1.call-update) | async-done | bytes 37748752 | tf_op jit(solution)/shard_map/all_gather | solution.py:44
  1266.6 48.7 %copy.42 = bf16[12288,1536]{1,0:T(8,128)(2,1)} copy(bf16[12288,1536]{0,1:T(8,128)(2,1)} %all-gather.9.cloned.1.call-done) | data formatting | bytes 75497472 | tf_op jit(solution)/shard_map/all_gather | solution.py:44
  1315.2 33.3 %gather_fusion.2 = bf16[120,128,1536]{2,1,0:T(8,128)(2,1)} fusion(bf16[96,128,1536]{2,1,0:T(8,128)(2,1)} %bitcast.86, s32[1024]{0:T(1024)S(1)} %copy-done.5), kind=kCustom, calls=%fused_computation.2.clone | custom fusion | bytes 94372320 | tf_op jit(solution)/shard_map/jit(_take)/gather | solution.py:13
  1348.5 24.3 %fusion.5 = f32[24,1536,128,1]{1,2,3,0:T(8,128)} fusion(bf16[24,5,128,128]{3,2,1,0:T(8,128)(2,1)} %param.12, bf16[24,5,128,1536]{3,2,1,0:T(8,128)(2,1)} %bitcast.92, pred[24,5]{1,0:T(8,128)(4,1)S(1)} %copy-done.15), kind=kOutput, calls=%fused_computation.9 | convolution fusion | flops 6063390720 | bytes 69992568 | tf_op jit(solution)/shard_map/jsoi,jsin->jon/dot_general | solution.py:14
  1372.8 18.7 copy.44
  1391.5 7.6 multiply_convert_fusion.1
  1399.1 212.8 %all_to_all.46 = bf16[8,384,1536]{1,2,0:T(8,128)(2,1)} all-to-all(bf16[8,384,1536]{1,2,0:T(8,128)(2,1)S(1)} %multiply_convert_fusion.1), channel_id=1, replica_groups=mesh['row'=8,'col'=4] {'row'}, dimensions={0} | all-to-all | bytes 18874368 | tf_op jit(solution)/shard_map/all_to_all | solution.py:46
  1611.9 12.6 copy.46
  1624.5 23.7 %gather_fusion.3 = bf16[480,384,128]{2,1,0:T(8,128)(2,1)} fusion(bf16[384,96,128]{2,0,1:T(8,128)(2,1)} %copy.46, s32[1024]{0:T(1024)S(1)} %copy-done.1), kind=kCustom, calls=%fused_computation.3.clone | custom fusion | bytes 94373760 | tf_op jit(solution)/shard_map/jit(_take)/gather | solution.py:22
  1648.2 31.3 %convert_reduce_fusion.1 = (f32[]{:T(128)}, f32[96,384,128,1]{1,2,3,0:T(8,128)}) fusion(f32[96,128]{1,0:T(8,128)S(1)} %copy-done.7, bf16[96,5,128,128]{3,2,1,0:T(8,128)(2,1)} %all-gather.7.cloned.1.call-done, bf16[96,5,384,128]{3,2,1,0:T(8,128)(2,1)} %bitcast.88, pred[96,5]{1,0:T(8,128)(4,1)S(1)} %copy-done.12), kind=kOutput, calls=%fused_computation.33 | convolution fusion | flops 6082265088 | bytes 81838560 | tf_op jit(solution)/shard_map/cisk,isok->cio/dot_general | solution.py:23
  1679.5 11.8 multiply_convert_fusion
  1696.4 226.1 %psum.23 = f32[]{:T(128)} all-reduce(f32[]{:T(128)} %get-tuple-element.13), channel_id=1, replica_groups=mesh['row'=8,'col'=4] {'row','col'}, use_global_device_ids=true, to_apply=%region_7.10 | all-reduce | flops 1 | bytes 8 | tf_op jit(solution)/shard_map/psum | solution.py:50
  1923.2 12.4 multiply_bitcast_fusion
  1935.5 7.6 copy.53
  1943.1 15.5 fusion.23
  (64 shorter events, 19.9 us)
Async XLA Ops:
  6.5 20.8 %copy-start.10 = (s32[24,5]{0,1:T(8,128)S(1)}, s32[24,5]{0,1:T(8,128)}, u32[]{:S(2)}) copy-start(s32[24,5]{0,1:T(8,128)} %param.13) | copy-start | bytes 1444
  6.5 250.1 %all-gather.5.cloned.1.call-start = ((), (), s32[]{:S(2)}) async-start(), calls=%async_computation.4 | async-start | bytes 47185920 | tf_op jit(solution)/shard_map/all_gather | solution.py:44
  26.6 666.9 %all-gather.7.cloned.1.call-start = ((), (), s32[]{:S(2)}) async-start(), calls=%async_computation.5 | async-start | bytes 17694720 | tf_op jit(solution)/shard_map/all_gather | solution.py:35
  27.4 311.4 %copy-start.14 = (pred[24,5]{1,0:T(8,128)(4,1)}, pred[24,5]{1,0:T(8,128)(4,1)S(1)}, u32[]{:S(2)}) copy-start(pred[24,5]{1,0:T(8,128)(4,1)S(1)} %copy.33) | copy-start | bytes 364
  30.4 353.5 %copy-start.8 = (f32[8,384]{1,0:T(8,128)}, f32[8,384]{1,0:T(8,128)S(1)}, u32[]{:S(2)}) copy-start(f32[8,384]{1,0:T(8,128)S(1)} %div.47) | copy-start | bytes 36868
  30.4 275.1 %copy-start.4 = (s32[1024]{0:T(1024)}, s32[1024]{0:T(1024)S(1)}, u32[]{:S(2)}) copy-start(s32[1024]{0:T(1024)S(1)} %pad_clamp_fusion.1) | copy-start | bytes 12292
  383.9 16.9 copy-start.13
  395.4 304.7 %all-to-all-start = ((bf16[8,384,1536]{1,2,0:T(8,128)(2,1)}), bf16[8,384,1536]{1,2,0:T(8,128)(2,1)}, u32[]{:S(2)}, u32[]{:S(2)}) async-start(bf16[8,384,1536]{1,2,0:T(8,128)(2,1)} %multiply_convert_fusion.3), calls=%async_computation | async-start | bytes 18874368 | tf_op jit(solution)/shard_map/all_to_all | solution.py:46
  693.1 43.3 %copy-start.11 = (pred[96,5]{1,0:T(8,128)(4,1)}, pred[96,5]{1,0:T(8,128)(4,1)S(1)}, u32[]{:S(2)}) copy-start(pred[96,5]{1,0:T(8,128)(4,1)S(1)} %copy.32) | copy-start | bytes 1444
  693.4 43.0 %copy-start = (s32[1024]{0:T(1024)}, s32[1024]{0:T(1024)S(1)}, u32[]{:S(2)}) copy-start(s32[1024]{0:T(1024)S(1)} %pad_clamp_fusion) | copy-start | bytes 12292
  700.1 36.3 %copy-start.6 = (f32[96,128]{1,0:T(8,128)}, f32[96,128]{1,0:T(8,128)S(1)}, u32[]{:S(2)}) copy-start(f32[96,128]{1,0:T(8,128)S(1)} %broadcast_divide_fusion) | copy-start | bytes 147460
  700.1 67.6 %copy-start.2 = (f32[8,1536]{1,0:T(8,128)}, f32[8,1536]{1,0:T(8,128)S(1)}, u32[]{:S(2)}) copy-start(f32[8,1536]{1,0:T(8,128)S(1)} %div.50) | copy-start | bytes 147460
  779.5 227.0 %all-to-all-start.1 = ((bf16[384,8,1536]{0,2,1:T(8,128)(2,1)}), bf16[384,8,1536]{0,2,1:T(8,128)(2,1)}, u32[]{:S(2)}, u32[]{:S(2)}) async-start(bf16[384,8,1536]{0,2,1:T(8,128)(2,1)} %multiply_convert_fusion.2), calls=%async_computation.1 | async-start | bytes 18874368 | tf_op jit(solution)/shard_map/all_to_all | solution.py:49
  784.6 482.0 %all-gather.9.cloned.1.call-start = ((), (), s32[]{:S(2)}) async-start(), calls=%async_computation.6 | async-start | bytes 47185920 | tf_op jit(solution)/shard_map/all_gather | solution.py:44
  1039.2 276.0 %copy-start.5 = (s32[1024]{0:T(1024)S(1)}, s32[1024]{0:T(1024)}, u32[]{:S(2)}) copy-start(s32[1024]{0:T(1024)} %copy-done.4) | copy-start | bytes 12292
  1315.2 33.3 %copy-start.15 = (pred[24,5]{1,0:T(8,128)(4,1)S(1)}, pred[24,5]{1,0:T(8,128)(4,1)}, u32[]{:S(2)}) copy-start(pred[24,5]{1,0:T(8,128)(4,1)} %copy-done.14) | copy-start | bytes 364
  1372.8 18.7 copy-start.9
  1399.1 225.5 %copy-start.1 = (s32[1024]{0:T(1024)S(1)}, s32[1024]{0:T(1024)}, u32[]{:S(2)}) copy-start(s32[1024]{0:T(1024)} %copy-done) | copy-start | bytes 12292
  1624.5 23.7 %copy-start.7 = (f32[96,128]{1,0:T(8,128)S(1)}, f32[96,128]{1,0:T(8,128)}, u32[]{:S(2)}) copy-start(f32[96,128]{1,0:T(8,128)} %copy-done.6) | copy-start | bytes 147460
  1624.5 23.7 %copy-start.12 = (pred[96,5]{1,0:T(8,128)(4,1)S(1)}, pred[96,5]{1,0:T(8,128)(4,1)}, u32[]{:S(2)}) copy-start(pred[96,5]{1,0:T(8,128)(4,1)} %copy-done.11) | copy-start | bytes 1444
  1648.2 31.3 %copy-start.3 = (f32[8,1536]{1,0:T(8,128)S(1)}, f32[8,1536]{1,0:T(8,128)}, u32[]{:S(2)}) copy-start(f32[8,1536]{1,0:T(8,128)} %copy-done.2) | copy-start | bytes 147460
  1691.3 231.9 %all-to-all-start.3 = ((bf16[384,8,1536]{0,2,1:T(8,128)(2,1)}), bf16[384,8,1536]{0,2,1:T(8,128)(2,1)}, u32[]{:S(2)}, u32[]{:S(2)}) async-start(bf16[384,8,1536]{0,2,1:T(8,128)(2,1)} %multiply_convert_fusion), calls=%async_computation.3 | async-start | bytes 18874368 | tf_op jit(solution)/shard_map/all_to_all | solution.py:49
Sparse Core Ops, SparseCore 0:
  26.7 229.8 all-gather.4
  258.8 288.7 all-gather.6
  1039.4 227.1 all-gather.8
where the time goes:
time: 1970 us
  blocking collectives  952 us (48%)
  waiting for transfers between devices  454 us (23%)
  local copies, waits for them, and re-layouts  290 us (15%)
  other arithmetic  125 us (6%)
  matrix products  113 us (6%)
    all_gather x2, waiting for transfers between devices, local(): gathered = lax.all_gather(current, 'col', axis=0, tiled=True)  454 us
    psum x2, blocking collectives, local(): slab_sum = lax.psum(partial_value, ('row', 'col'))  447 us
    all_gather x1, blocking collectives, local(): lax.all_gather(columns_first, 'row', axis=0, tiled=True)  292 us
    all_to_all x1, blocking collectives, local(): lax.all_to_all(mixed_cols, 'row', split_axis=0, concat_axis=1, tiled=True)  213 us
    all_gather x2, local copies, waits for them, and re-layouts, local(): gathered = lax.all_gather(current, 'col', axis=0, tiled=True)  97.6 us
    gather x2, local copies, waits for them, and re-layouts, second_product(): picked = jnp.take(blocks, columns, axis=0)  66.5 us
    dot_general x2, matrix products, first_product(): jnp.einsum('cisk,isok->cio', picked, tile_set, preferred_element_type=jnp...  62.6 us
    dot_general x2, matrix products, second_product(): jnp.einsum('jsoi,jsin->jon', tile_set, picked, preferred_element_type=jnp...  50.7 us
  transfers between devices with their start and end apart: 6, of which 2 were waited for; matrix products, arithmetic and copies ran while one was open for 8% of the time, Pallas kernels for 0%

commit v1 on v0

--- a/solution.py
+++ b/solution.py
@@ -2,6 +2,7 @@
 import jax.numpy as jnp
 from jax import lax
 from jax.sharding import PartitionSpec as P
+from jax.lax import all_to_all, axis_size
 
 ITERS = 2
 mixing = 0.8
@@ -43,7 +44,11 @@
         current = current_state.astype(jnp.bfloat16)
         gathered = lax.all_gather(current, "col", axis=0, tiled=True)
         mixed_cols = second_product(gathered, tiles_second, columns_second, inverse_second)
-        slab_data = lax.all_to_all(mixed_cols, "row", split_axis=0, concat_axis=1, tiled=True)
+        v_next = axis_size("row")
+        extra = jnp.split(mixed_cols, v_next, axis=0)
+        arr_next = jnp.stack(extra)
+        u1 = all_to_all(arr_next, "row", 0, 0)
+        slab_data = jnp.concatenate(u1, axis=1)
         propagated = first_product(slab_data, all_first, all_columns, inverse_first)
         partial_value = jnp.sum(propagated.astype(jnp.float32))
         returned = lax.all_to_all(propagated, "row", split_axis=1, concat_axis=0, tiled=True)

time: 1970 us -> 1970 us (level)
    another operation x0 -> x4, local copies, waits for them, and re-layouts: none -> 26.7 us  [the longest x2 25.2 us: first_product(): blocks = slab_data.reshape(slab_data.shape[0], -1, tile_size)]
    reshape x2 -> x0, local copies, waits for them, and re-layouts: 25.2 us -> none  [first_product(): blocks = slab_data.reshape(slab_data.shape[0], -1, tile_size)]
where the time goes in v1:
time: 1970 us
  blocking collectives  946 us (48%)
  waiting for transfers between devices  454 us (23%)
  local copies, waits for them, and re-layouts  302 us (15%)
  other arithmetic  121 us (6%)
  matrix products  113 us (6%)
    all_gather x2, waiting for transfers between devices, local(): gathered = lax.all_gather(current, 'col', axis=0, tiled=True)  454 us
    psum x2, blocking collectives, local(): slab_sum = lax.psum(partial_value, ('row', 'col'))  447 us
    all_gather x1, blocking collectives, local(): lax.all_gather(columns_first, 'row', axis=0, tiled=True)  286 us
    all_to_all x1, blocking collectives, local(): u1 = all_to_all(arr_next, 'row', 0, 0)  213 us
    all_gather x2, local copies, waits for them, and re-layouts, local(): gathered = lax.all_gather(current, 'col', axis=0, tiled=True)  97.6 us
    gather x2, local copies, waits for them, and re-layouts, second_product(): picked = jnp.take(blocks, columns, axis=0)  66.5 us
    dot_general x2, matrix products, first_product(): jnp.einsum('cisk,isok->cio', picked, tile_set, preferred_element_type=jnp...  62.6 us
    dot_general x2, matrix products, second_product(): jnp.einsum('jsoi,jsin->jon', tile_set, picked, preferred_element_type=jnp...  50.7 us
  transfers between devices with their start and end apart: 6, of which 2 were waited for; matrix products, arithmetic and copies ran while one was open for 8% of the time, Pallas kernels for 0%

profile of v1, /device:TPU:0, one launch (start us, length us, event | category | flops | bytes accessed | tf_op | source)
XLA Modules:
  0.0 1967.5 jit_solution(2612123066868449828)
XLA Ops:
  6.5 20.0 %fusion.44 = (f32[]{:T(128)}, bf16[3072,1536]{0,1:T(8,128)(2,1)}) fusion(f32[1536,3072]{1,0:T(8,128)} %param.9), kind=kLoop, calls=%fused_computation.87 | loop fusion | flops 9437183 | bytes 28311556 | tf_op jit(solution)/shard_map/reduce_sum | solution.py:41
  30.4 226.2 %all-gather.5.cloned.1.call-done = bf16[12288,1536]{0,1:T(8,128)(2,1)} async-done(((bf16[3072,1536]{0,1:T(8,128)(2,1)}), bf16[12288,1536]{0,1:T(8,128)(2,1)}) %all-gather.5.cloned.1.call-update) | async-done | bytes 37748752 | tf_op jit(solution)/shard_map/all_gather | solution.py:45
  256.6 48.9 %copy.36 = bf16[12288,1536]{1,0:T(8,128)(2,1)} copy(bf16[12288,1536]{0,1:T(8,128)(2,1)} %all-gather.5.cloned.1.call-done) | data formatting | bytes 75497472 | tf_op jit(solution)/shard_map/all_gather | solution.py:45
  305.5 33.3 %gather_fusion = bf16[120,128,1536]{2,1,0:T(8,128)(2,1)} fusion(bf16[96,128,1536]{2,1,0:T(8,128)(2,1)} %bitcast.153, s32[1024]{0:T(1024)S(1)} %pad_clamp_fusion.1), kind=kCustom, calls=%fused_computation.clone | custom fusion | bytes 94372320 | tf_op jit(solution)/shard_map/jit(_take)/gather | solution.py:14
  338.8 26.4 %fusion.8 = f32[24,1536,128,1]{1,2,3,0:T(8,128)} fusion(bf16[24,5,128,128]{3,2,1,0:T(8,128)(2,1)} %param.12, bf16[24,5,128,1536]{3,2,1,0:T(8,128)(2,1)} %bitcast.159, pred[24,5]{1,0:T(8,128)(4,1)S(1)} %copy.33), kind=kOutput, calls=%fused_computation.12 | convolution fusion | flops 6063390720 | bytes 69992568 | tf_op jit(solution)/shard_map/jsoi,jsin->jon/dot_general | solution.py:15
  365.2 18.7 copy.38
  383.9 7.7 multiply_convert_fusion.3
  406.6 286.3 %all-gather = s32[8,12,5]{1,2,0:T(8,128)S(1)} all-gather(s32[1,12,5]{1,2,0:T(8,128)S(1)} %bitcast.165), channel_id=1, replica_groups=mesh['row'=8,'col'=4] {'row'}, dimensions={0}, use_global_device_ids=true | all-gather | bytes 2160 | tf_op jit(solution)/shard_map/all_gather | solution.py:37
  693.5 6.6 convert_reduce_fusion
  700.2 12.6 copy.40
  712.8 23.6 %gather_fusion.1 = bf16[480,384,128]{2,1,0:T(8,128)(2,1)} fusion(bf16[384,96,128]{2,0,1:T(8,128)(2,1)} %copy.40, s32[1024]{0:T(1024)S(1)} %pad_clamp_fusion), kind=kCustom, calls=%fused_computation.1.clone | custom fusion | bytes 94373760 | tf_op jit(solution)/shard_map/jit(_take)/gather | solution.py:23
  736.4 31.3 %convert_reduce_fusion.2 = (f32[]{:T(128)}, f32[96,384,128,1]{1,2,3,0:T(8,128)}) fusion(f32[96,128]{1,0:T(8,128)S(1)} %broadcast_divide_fusion, bf16[96,5,128,128]{3,2,1,0:T(8,128)(2,1)} %all-gather.7.cloned.1.call-done, bf16[96,5,384,128]{3,2,1,0:T(8,128)(2,1)} %bitcast.155, pred[96,5]{1,0:T(8,128)(4,1)S(1)} %copy.32), kind=kOutput, calls=%fused_computation.37 | convolution fusion | flops 6082265088 | bytes 81838560 | tf_op jit(solution)/shard_map/cisk,isok->cio/dot_general | solution.py:24
  767.7 11.8 multiply_convert_fusion.2
  784.6 220.6 %all-reduce = (f32[]{:T(128)}, f32[]{:T(128)}) all-reduce(f32[]{:T(128)} %get-tuple-element.11, f32[]{:T(128)} %get-tuple-element.9), channel_id=1, replica_groups=mesh['row'=8,'col'=4] {'row','col'}, use_global_device_ids=true, to_apply=%region_3.6 | all-reduce | flops 2 | bytes 16 | tf_op jit(solution)/shard_map/psum | solution.py:55
  1006.5 12.4 multiply_bitcast_fusion.1
  1018.9 7.6 copy.52
  1026.5 12.7 fusion.21
  1039.2 227.3 %all-gather.9.cloned.1.call-done = bf16[12288,1536]{0,1:T(8,128)(2,1)} async-done(((bf16[3072,1536]{0,1:T(8,128)(2,1)}), bf16[12288,1536]{0,1:T(8,128)(2,1)}) %all-gather.9.cloned.1.call-update) | async-done | bytes 37748752 | tf_op jit(solution)/shard_map/all_gather | solution.py:45
  1266.6 48.7 %copy.42 = bf16[12288,1536]{1,0:T(8,128)(2,1)} copy(bf16[12288,1536]{0,1:T(8,128)(2,1)} %all-gather.9.cloned.1.call-done) | data formatting | bytes 75497472 | tf_op jit(solution)/shard_map/all_gather | solution.py:45
  1315.2 33.3 %gather_fusion.2 = bf16[120,128,1536]{2,1,0:T(8,128)(2,1)} fusion(bf16[96,128,1536]{2,1,0:T(8,128)(2,1)} %bitcast.152, s32[1024]{0:T(1024)S(1)} %copy-done.5), kind=kCustom, calls=%fused_computation.2.clone | custom fusion | bytes 94372320 | tf_op jit(solution)/shard_map/jit(_take)/gather | solution.py:14
  1348.5 24.3 %fusion.5 = f32[24,1536,128,1]{1,2,3,0:T(8,128)} fusion(bf16[24,5,128,128]{3,2,1,0:T(8,128)(2,1)} %param.12, bf16[24,5,128,1536]{3,2,1,0:T(8,128)(2,1)} %bitcast.158, pred[24,5]{1,0:T(8,128)(4,1)S(1)} %copy-done.15), kind=kOutput, calls=%fused_computation.9 | convolution fusion | flops 6063390720 | bytes 69992568 | tf_op jit(solution)/shard_map/jsoi,jsin->jon/dot_general | solution.py:15
  1372.8 18.7 copy.44
  1391.5 7.7 multiply_convert_fusion.1
  1401.3 212.8 %all_to_all.30 = bf16[8,384,1536]{1,2,0:T(8,128)(2,1)} all-to-all(bf16[8,384,1536]{1,2,0:T(8,128)(2,1)S(1)} %fusion.24), channel_id=1, replica_groups=mesh['row'=8,'col'=4] {'row'}, dimensions={0} | all-to-all | bytes 18874368 | tf_op jit(solution)/shard_map/all_to_all | solution.py:50
  1614.2 12.6 copy.46
  1626.8 23.7 %gather_fusion.3 = bf16[480,384,128]{2,1,0:T(8,128)(2,1)} fusion(bf16[384,96,128]{2,0,1:T(8,128)(2,1)} %copy.46, s32[1024]{0:T(1024)S(1)} %copy-done.1), kind=kCustom, calls=%fused_computation.3.clone | custom fusion | bytes 94373760 | tf_op jit(solution)/shard_map/jit(_take)/gather | solution.py:23
  1650.5 31.3 %convert_reduce_fusion.1 = (f32[]{:T(128)}, f32[96,384,128,1]{1,2,3,0:T(8,128)}) fusion(f32[96,128]{1,0:T(8,128)S(1)} %copy-done.7, bf16[96,5,128,128]{3,2,1,0:T(8,128)(2,1)} %all-gather.7.cloned.1.call-done, bf16[96,5,384,128]{3,2,1,0:T(8,128)(2,1)} %bitcast.154, pred[96,5]{1,0:T(8,128)(4,1)S(1)} %copy-done.12), kind=kOutput, calls=%fused_computation.33 | convolution fusion | flops 6082265088 | bytes 81838560 | tf_op jit(solution)/shard_map/cisk,isok->cio/dot_general | solution.py:24
  1681.8 11.8 multiply_convert_fusion
  1698.7 226.1 %psum.23 = f32[]{:T(128)} all-reduce(f32[]{:T(128)} %get-tuple-element.13), channel_id=1, replica_groups=mesh['row'=8,'col'=4] {'row','col'}, use_global_device_ids=true, to_apply=%region_7.10 | all-reduce | flops 1 | bytes 8 | tf_op jit(solution)/shard_map/psum | solution.py:55
  1925.5 12.4 multiply_bitcast_fusion
  1937.8 7.6 copy.53
  1945.4 15.5 fusion.23
  (79 shorter events, 31.7 us)
Async XLA Ops:
  6.5 250.1 %all-gather.5.cloned.1.call-start = ((), (), s32[]{:S(2)}) async-start(), calls=%async_computation.4 | async-start | bytes 47185920 | tf_op jit(solution)/shard_map/all_gather | solution.py:45
  26.5 0.8 copy-start.10
  26.6 666.9 %all-gather.7.cloned.1.call-start = ((), (), s32[]{:S(2)}) async-start(), calls=%async_computation.5 | async-start | bytes 17694720 | tf_op jit(solution)/shard_map/all_gather | solution.py:36
  27.4 311.4 %copy-start.14 = (pred[24,5]{1,0:T(8,128)(4,1)}, pred[24,5]{1,0:T(8,128)(4,1)S(1)}, u32[]{:S(2)}) copy-start(pred[24,5]{1,0:T(8,128)(4,1)S(1)} %copy.33) | copy-start | bytes 364
  27.7 277.9 %copy-start.4 = (s32[1024]{0:T(1024)}, s32[1024]{0:T(1024)S(1)}, u32[]{:S(2)}) copy-start(s32[1024]{0:T(1024)S(1)} %pad_clamp_fusion.1) | copy-start | bytes 12292
  30.4 353.5 %copy-start.8 = (f32[3072]{0:T(1024)}, f32[3072]{0:T(1024)S(1)}, u32[]{:S(2)}) copy-start(f32[3072]{0:T(1024)S(1)} %divide_bitcast_fusion) | copy-start | bytes 36868
  401.1 5.5 copy-start.13
  401.1 299.0 %all-to-all-start = ((bf16[8,384,1536]{1,2,0:T(8,128)(2,1)}), bf16[8,384,1536]{1,2,0:T(8,128)(2,1)}, u32[]{:S(2)}, u32[]{:S(2)}) async-start(bf16[8,384,1536]{1,2,0:T(8,128)(2,1)} %fusion.32), calls=%async_computation | async-start | bytes 18874368 | tf_op jit(solution)/shard_map/all_to_all | solution.py:50
  693.1 43.3 %copy-start.11 = (pred[96,5]{1,0:T(8,128)(4,1)}, pred[96,5]{1,0:T(8,128)(4,1)S(1)}, u32[]{:S(2)}) copy-start(pred[96,5]{1,0:T(8,128)(4,1)S(1)} %copy.32) | copy-start | bytes 1444
  693.4 19.3 copy-start
  700.1 36.3 %copy-start.6 = (f32[96,128]{1,0:T(8,128)}, f32[96,128]{1,0:T(8,128)S(1)}, u32[]{:S(2)}) copy-start(f32[96,128]{1,0:T(8,128)S(1)} %broadcast_divide_fusion) | copy-start | bytes 147460
  700.1 67.5 %copy-start.2 = (f32[8,1536]{1,0:T(8,128)}, f32[8,1536]{1,0:T(8,128)S(1)}, u32[]{:S(2)}) copy-start(f32[8,1536]{1,0:T(8,128)S(1)} %div.50) | copy-start | bytes 147460
  779.5 227.0 %all-to-all-start.1 = ((bf16[384,8,1536]{0,2,1:T(8,128)(2,1)}), bf16[384,8,1536]{0,2,1:T(8,128)(2,1)}, u32[]{:S(2)}, u32[]{:S(2)}) async-start(bf16[384,8,1536]{0,2,1:T(8,128)(2,1)} %multiply_convert_fusion.2), calls=%async_computation.1 | async-start | bytes 18874368 | tf_op jit(solution)/shard_map/all_to_all | solution.py:54
  784.6 482.0 %all-gather.9.cloned.1.call-start = ((), (), s32[]{:S(2)}) async-start(), calls=%async_computation.6 | async-start | bytes 47185920 | tf_op jit(solution)/shard_map/all_gather | solution.py:45
  1039.2 276.0 %copy-start.5 = (s32[1024]{0:T(1024)S(1)}, s32[1024]{0:T(1024)}, u32[]{:S(2)}) copy-start(s32[1024]{0:T(1024)} %copy-done.4) | copy-start | bytes 12292
  1315.2 33.3 %copy-start.15 = (pred[24,5]{1,0:T(8,128)(4,1)S(1)}, pred[24,5]{1,0:T(8,128)(4,1)}, u32[]{:S(2)}) copy-start(pred[24,5]{1,0:T(8,128)(4,1)} %copy-done.14) | copy-start | bytes 364
  1372.8 18.7 copy-start.9
  1614.2 12.6 copy-start.1
  1626.8 23.7 %copy-start.7 = (f32[96,128]{1,0:T(8,128)S(1)}, f32[96,128]{1,0:T(8,128)}, u32[]{:S(2)}) copy-start(f32[96,128]{1,0:T(8,128)} %copy-done.6) | copy-start | bytes 147460
  1626.8 23.7 %copy-start.12 = (pred[96,5]{1,0:T(8,128)(4,1)S(1)}, pred[96,5]{1,0:T(8,128)(4,1)}, u32[]{:S(2)}) copy-start(pred[96,5]{1,0:T(8,128)(4,1)} %copy-done.11) | copy-start | bytes 1444
  1650.5 31.3 %copy-start.3 = (f32[8,1536]{1,0:T(8,128)S(1)}, f32[8,1536]{1,0:T(8,128)}, u32[]{:S(2)}) copy-start(f32[8,1536]{1,0:T(8,128)} %copy-done.2) | copy-start | bytes 147460
  1693.6 231.9 %all-to-all-start.3 = ((bf16[384,8,1536]{0,2,1:T(8,128)(2,1)}), bf16[384,8,1536]{0,2,1:T(8,128)(2,1)}, u32[]{:S(2)}, u32[]{:S(2)}) async-start(bf16[384,8,1536]{0,2,1:T(8,128)(2,1)} %multiply_convert_fusion), calls=%async_computation.3 | async-start | bytes 18874368 | tf_op jit(solution)/shard_map/all_to_all | solution.py:54
Sparse Core Ops, SparseCore 0:
  26.7 229.8 all-gather.4
  258.8 365.1 all-gather.6
  1039.3 227.1 all-gather.8
